TPU v7x, 32 devices: a whole 2x2x4 slice. The times are simulated.
32 devices in a mesh: grp: 8 (over z, y), slab: 4 (over x, core).
Axes of the slice: x: 2, y: 2, z: 4, core: 2. Of those that a mesh axis runs over, the one named last changes fastest.
Arguments:
- grids: float32 [8, 512, 4096], P('grp', 'slab'), may hold values from -6 to 6
- first_level: int32 [8], P('grp'), may hold values from 6 to 8, as said below
- coeffs: int32 [8], P('grp'), may hold values from -3 to 3
- slot_map: int32 [8, 512], P('grp', 'slab'), may hold values from 0 to 1023, as said below
Outputs:
- combined_grid: float32 [8, 512, 4096], P('grp', 'slab')
Inputs may be any that keep to these rules, and one draw needn't show every extreme that they name: The second dimension of grid g has level 9 minus first_level[g]. Every value of the range is taken by some grid. `slot_map`: grid g's point with first coordinate i of 2^a points lies at position i / 2^a of a periodic unit interval, and likewise in the second dimension. Two rows of any grids at the same position in the first two dimensions share a slot; rows of one grid have distinct slots; every slot is used by some grid. The rows held by the s-th index of slab (first coordinates in the s-th of 4 equal ranges) of every grid have slots in the s-th of 4 equal aligned ranges of the 1024 slots.
All inputs are finite; a program needn't handle non-finite values.
Results may differ from a plain program's by a relative error of at most 0.0003.
Values sent between devices are 32-bit elements; how exact they have to be, the bound alone decides.
A program may use at most 64 MiB of HBM per device.

v0:
```python
import jax
import jax.numpy as jnp
from jax import lax
from jax.sharding import PartitionSpec as P

P2 = 16
P3 = 16
P4 = 16
LEVEL_SUM = 9
PLANE = 8
ROWS = 512


def hier_weight(target, source, period):
    spread = target & -target
    interior = (target != 0).astype(jnp.float32)
    left_side = (source == target - spread).astype(jnp.float32)
    right_side = (source == (target + spread) % period).astype(jnp.float32)
    return (target == source).astype(jnp.float32) - 0.5 * interior * (left_side + right_side)


def dehier_weight(target, source, period):
    spread = jnp.maximum(source & -source, 1).astype(jnp.float32)
    apart = jnp.abs(target - source)
    apart = jnp.minimum(apart, period - apart).astype(jnp.float32)
    return jnp.where(source == 0, 1.0, jnp.maximum(0.0, 1.0 - apart / spread))


def square_table(maker, length):
    points = jnp.arange(length, dtype=jnp.int32)
    return maker(points[:, None], points[None, :], length)


def inner_apply(values, third_op, rest_op):
    count = values.shape[0]
    shaped = values.reshape(count, P2, P3 * P4)
    shaped = jnp.einsum("ij,rjk->rik", third_op, shaped, precision=lax.Precision.HIGHEST)
    shaped = jnp.einsum("rjk,lk->rjl", shaped, rest_op, precision=lax.Precision.HIGHEST)
    return shaped.reshape(count, P2 * P3 * P4)


def exact_dot(left, right):
    return jnp.dot(left, right, precision=lax.Precision.HIGHEST, preferred_element_type=jnp.float32)


def shards(grids, first_level, coeffs, slot_map):
    grid_rows = grids[0]
    level = first_level[0]
    second = LEVEL_SUM - level
    rows_dev = grid_rows.shape[0]
    width = grid_rows.shape[1]
    slabs = lax.axis_size("slab")
    slab_index = lax.axis_index("slab")
    span = rows_dev >> second
    row_ids = jnp.arange(rows_dev, dtype=jnp.int32)
    first_pos = row_ids >> second
    second_pos = row_ids & (1 << second) - 1
    slab_ids = jnp.arange(slabs, dtype=jnp.int32)
    same_first = (first_pos[:, None] == first_pos[None, :]).astype(jnp.float32)
    hier_third = square_table(hier_weight, P2)
    hier_rest = jnp.kron(square_table(hier_weight, P3), square_table(hier_weight, P4))
    values = inner_apply(grid_rows, hier_third, hier_rest)
    second_op = same_first * hier_weight(second_pos[:, None], second_pos[None, :], 1 << second)
    values = exact_dot(second_op, values)
    plane = values[:PLANE]
    planes = lax.all_gather(plane[None], "slab", axis=0, tiled=True)
    following = lax.dynamic_index_in_dim(planes, (slab_index + 1) % slabs, 0, keepdims=False)
    extended = jnp.concatenate([values, following], axis=0)
    ext_ids = jnp.arange(rows_dev + PLANE, dtype=jnp.int32)
    ext_first = ext_ids >> second
    ext_second = ext_ids & (1 << second) - 1
    spread = first_pos & -first_pos
    interior = (first_pos != 0).astype(jnp.float32)[:, None]
    same_second = (second_pos[:, None] == ext_second[None, :]).astype(jnp.float32)
    centre = (ext_first[None, :] == first_pos[:, None]).astype(jnp.float32)
    below = (ext_first[None, :] == (first_pos - spread)[:, None]).astype(jnp.float32)
    above = (ext_first[None, :] == (first_pos + spread)[:, None]).astype(jnp.float32)
    fine_op = same_second * (centre - 0.5 * interior * (below + above))
    surplus = exact_dot(fine_op, extended)
    coarse_weights = hier_weight(slab_index, slab_ids, slabs)
    coarse = jnp.einsum("q,qpk->pk", coarse_weights, planes, precision=lax.Precision.HIGHEST)
    padded = jnp.concatenate([coarse, jnp.zeros((rows_dev - PLANE, width), jnp.float32)], axis=0)
    surplus = jnp.where((first_pos == 0)[:, None], padded, surplus)
    scaled = coeffs[0].astype(jnp.float32) * surplus
    per_slab = 2 * ROWS // slabs
    slot_local = slot_map[0] % per_slab
    slot_ids = jnp.arange(per_slab, dtype=jnp.int32)
    gather_op = (slot_local[None, :] == slot_ids[:, None]).astype(jnp.float32)
    term = exact_dot(gather_op, scaled)
    total = lax.psum(term, "grp")
    spread_op = (slot_local[:, None] == slot_ids[None, :]).astype(jnp.float32)
    combined = exact_dot(spread_op, total)
    back_third = square_table(dehier_weight, P2)
    back_rest = jnp.kron(square_table(dehier_weight, P3), square_table(dehier_weight, P4))
    values = inner_apply(combined, back_third, back_rest)
    back_second = same_first * dehier_weight(second_pos[:, None], second_pos[None, :], 1 << second)
    values = exact_dot(back_second, values)
    top_plane = values[:PLANE]
    top_planes = lax.all_gather(top_plane[None], "slab", axis=0, tiled=True)
    here_weights = dehier_weight(slab_index, slab_ids, slabs)
    there_weights = dehier_weight((slab_index + 1) % slabs, slab_ids, slabs)
    here = jnp.einsum("q,qpk->pk", here_weights, top_planes, precision=lax.Precision.HIGHEST)
    there = jnp.einsum("q,qpk->pk", there_weights, top_planes, precision=lax.Precision.HIGHEST)
    same_row_second = (second_pos[:, None] == second_pos[None, :]).astype(jnp.float32)
    inside = (first_pos[None, :] != 0).astype(jnp.float32)
    local_op = (
        same_row_second * inside * dehier_weight(first_pos[:, None], first_pos[None, :], 2 * span)
    )
    fraction = first_pos.astype(jnp.float32) / span.astype(jnp.float32)
    plane_ids = jnp.arange(PLANE, dtype=jnp.int32)
    plane_pick = (second_pos[:, None] == plane_ids[None, :]).astype(jnp.float32)
    nodal = exact_dot(local_op, values)
    nodal = nodal + exact_dot((1.0 - fraction)[:, None] * plane_pick, here)
    nodal = nodal + exact_dot(fraction[:, None] * plane_pick, there)
    return nodal[None]


def solution(mesh):
    in_specs = (P("grp", "slab", None), P("grp"), P("grp"), P("grp", "slab"))
    out_specs = P("grp", "slab", None)
    return jax.shard_map(shards, mesh=mesh, in_specs=in_specs, out_specs=out_specs, check_vma=False)
```

profile of v0, /device:TPU:0, one launch (start us, length us, event | category | flops | bytes accessed | tf_op | source)
XLA Modules:
  0.0 230.8 jit_solution(8167477807761341772)
XLA Ops:
  6.5 0.0 all-reduce.3.cloned.1.call-start
  7.3 0.1 and_select_fusion.1
  7.5 2.3 copy.16
  9.7 0.1 multiply_subtract_fusion
  9.8 1.9 fusion.114
  11.8 1.5 broadcast_multiply_fusion.1
  13.3 2.4 %reshape.448 = f32[256,256,1]{1,0,2:T(8,128)S(1)} reshape(f32[16,16,16,16]{3,2,1,0:T(8,128)} %broadcast_multiply_fusion.1) | data formatting | bytes 524288 | tf_op jit(solution)/shard_map/jit(kron)/mul | solution.py:61
  15.7 3.2 %fusion.7 = f32[128,16,256]{0,2,1:T(8,128)S(1)} fusion(f32[256,256,1]{1,0,2:T(8,128)S(1)} %reshape.448, f32[16,128,256]{2,0,1:T(8,128)S(1)} %fusion.114), kind=kOutput, calls=%fused_computation.10 | convolution fusion | flops 1610612736 | bytes 4456448 | tf_op jit(solution)/shard_map/rjk,lk->rjl/dot_general | solution.py:38
  19.0 2.0 fusion.39
  21.0 0.0 copy-start
  21.0 8.8 %all-gather = f32[32,4096]{1,0:T(8,128)S(1)} all-gather(f32[8,4096]{1,0:T(8,128)S(1)} %slice.8), channel_id=2, replica_groups=mesh['grp'=8,'slab'=4] {'slab'}, dimensions={0}, use_global_device_ids=true | all-gather | bytes 655360 | tf_op jit(solution)/shard_map/all_gather | solution.py:66
  29.8 1.2 fusion.11
  31.1 0.1 copy.41
  31.8 0.0 copy-done
  31.8 2.1 fusion.1
  33.9 3.9 %fusion.29 = f32[256,4096]{1,0:T(8,128)} fusion(f32[128,4096]{1,0:T(8,128)S(1)} %fusion.1, s32[128]{0:T(128)S(1)} %fusion.130), kind=kOutput, calls=%fused_computation.38 | convolution fusion | flops 1610645504 | bytes 6291968 | tf_op jit(solution)/shard_map/dot_general | solution.py:43
  37.8 0.0 all-reduce.3.cloned.1.call-update
  37.9 0.2 broadcast_multiply_fusion
  38.1 0.9 reshape.452
  39.1 156.1 %all-reduce.3.cloned.1.call-done = f32[256,4096]{1,0:T(8,128)} async-done(((f32[256,4096]{1,0:T(8,128)}), f32[256,4096]{1,0:T(8,128)}) %all-reduce.3.cloned.1.call-update) | async-done | bytes 4194320 | tf_op jit(solution)/shard_map/psum | solution.py:90
  195.2 3.9 %fusion.28 = f32[128,4096]{1,0:T(8,128)S(1)} fusion(f32[256,4096]{1,0:T(8,128)} %all-reduce.3.cloned.1.call-done, s32[128]{0:T(128)S(1)} %and_select_fusion.3), kind=kOutput, calls=%fused_computation.37 | convolution fusion | flops 1610645504 | bytes 6291968 | tf_op jit(solution)/shard_map/dot_general | solution.py:43
  199.1 0.7 copy.17
  199.8 1.9 fusion.112
  201.7 3.5 %fusion.5 = f32[128,16,256]{0,2,1:T(8,128)S(1)} fusion(f32[256,256,1]{1,0,2:T(8,128)S(1)} %reshape.452, f32[128,256,16]{1,2,0:T(8,128)S(1)} %fusion.112), kind=kOutput, calls=%fused_computation.8 | convolution fusion | flops 1610612736 | bytes 4456448 | tf_op jit(solution)/shard_map/rjk,lk->rjl/dot_general | solution.py:38
  205.2 2.0 fusion.38
  207.2 7.1 %all-gather.1 = f32[32,4096]{1,0:T(8,128)S(1)} all-gather(f32[8,4096]{1,0:T(8,128)S(1)} %slice.9), channel_id=3, replica_groups=mesh['grp'=8,'slab'=4] {'slab'}, dimensions={0}, use_global_device_ids=true | all-gather | bytes 655360 | tf_op jit(solution)/shard_map/all_gather | solution.py:99
  214.4 1.3 fusion.15
  215.6 1.3 fusion.13
  216.9 2.0 fusion.35
  218.9 1.9 convolution_add_fusion.1
  220.8 3.2 %fusion = f32[1,128,4096]{2,1,0:T(8,128)} fusion(f32[128,4096]{1,0:T(8,128)S(1)} %convolution_add_fusion.1, f32[1,8,4096]{2,0,1:T(1,128)S(1)} %fusion.13, f32[128]{0:T(128)S(1)} %get-tuple-element.6, s32[128]{0:T(128)S(1)} %get-tuple-element.13), kind=kOutput, calls=%fused_computation.1 | convolution fusion | flops 50857984 | bytes 4326400 | tf_op jit(solution)/shard_map/dot_general | solution.py:43
  (21 shorter events, 0.2 us)
Async XLA Ops:
  6.5 188.7 %all-reduce.3.cloned.1.call-start = ((), (), s32[]{:S(2)}) async-start(), calls=%async_computation | async-start | bytes 8388608 | tf_op jit(solution)/shard_map/psum | solution.py:90
  21.0 10.9 %copy-start = (s32[1,128]{1,0:T(1,128)S(1)}, s32[1,128]{1,0:T(1,128)}, u32[]{:S(2)}) copy-start(s32[1,128]{1,0:T(1,128)} %param.7) | copy-start | bytes 1540
Sparse Core Ops, SparseCore 0:
  37.9 157.2 all-reduce.2
where the time goes:
time: 231 us
  waiting for transfers between devices  156 us (68%)
  matrix products  35.2 us (15%)
  blocking collectives  16 us (7%)
  between operations  15 us (6%)
  local copies, waits for them, and re-layouts  6.43 us (3%)
    psum x1, waiting for transfers between devices, shards(): total = lax.psum(term, 'grp')  156 us
    dot_general x8, matrix products, exact_dot(): jnp.dot(left, right, precision=lax.Precision.HIGHEST, preferred_element_t...  20.9 us
    all_gather x1, blocking collectives, shards(): planes = lax.all_gather(plane[None], 'slab', axis=0, tiled=True)  8.82 us
    all_gather x1, blocking collectives, shards(): top_planes = lax.all_gather(top_plane[None], 'slab', axis=0, tiled=True)  7.14 us
    dot_general x2, matrix products, inner_apply(): jnp.einsum('rjk,lk->rjl', shaped, rest_op, precision=lax.Precision.HIGHEST)  6.7 us
  transfers between devices with their start and end apart: 1, of which 1 were waited for; matrix products, arithmetic and copies ran while one was open for 1% of the time, Pallas kernels for 0%

commit v1 on v0

--- a/solution.py
+++ b/solution.py
@@ -1,6 +1,10 @@
+import functools
+
 import jax
 import jax.numpy as jnp
 from jax import lax
+from jax.experimental import pallas as pl
+from jax.experimental.pallas import tpu as pltpu
 from jax.sharding import PartitionSpec as P
 
 P2 = 16
@@ -9,6 +13,7 @@
 LEVEL_SUM = 9
 PLANE = 8
 ROWS = 512
+MESH = pl.DeviceIdType.MESH
 
 
 def hier_weight(target, source, period):
@@ -115,7 +120,269 @@
     return nodal[None]
 
 
+HALVES = 2
+LANES = 128
+
+
+def split_pair(values):
+    high = values.astype(jnp.bfloat16)
+    low = (values - high.astype(jnp.float32)).astype(jnp.bfloat16)
+    return high, low
+
+
+def mix(weights, body, edge):
+    body_high, body_low = split_pair(body)
+    edge_high, edge_low = split_pair(edge)
+    stacked = jnp.concatenate([body_high, body_low, edge_high, edge_low], axis=0)
+    return jnp.dot(weights, stacked, preferred_element_type=jnp.float32)
+
+
+def kernel(groups, slabs, per_slab, grid_ref, slot_ref, fwd_ref, back_ref, out_ref,
+           sent, got, table, spread, back, vals, planes, tops, slots, pick, place,
+           plane_send, plane_recv, slot_send, slot_recv, fwd_send, fwd_recv,
+           back_send, back_recv, top_send, top_recv):
+    me = lax.axis_index("grp")
+    here = lax.axis_index("slab")
+    rows = grid_ref.shape[0]
+    piece = sent.shape[3]
+    chunk = HALVES * piece
+
+    def group_at(step):
+        return lax.rem(me + step, groups)
+
+    def slab_at(step):
+        return lax.rem(here + step, slabs)
+
+    def columns(owner, half):
+        return pl.ds(pl.multiple_of(owner * chunk + half * piece, piece), piece)
+
+    barrier = pltpu.get_barrier_semaphore()
+    for step in range(1, groups):
+        pl.semaphore_signal(barrier, inc=1, device_id={"grp": group_at(step)}, device_id_type=MESH)
+    for step in range(1, slabs):
+        pl.semaphore_signal(barrier, inc=1, device_id={"slab": slab_at(step)}, device_id_type=MESH)
+    pl.semaphore_wait(barrier, groups + slabs - 2)
+
+    order = list(range(1, groups)) + [0]
+    pending = []
+
+    def plane_copy(half, step, away):
+        cols = columns(group_at(step), half)
+        return pltpu.make_async_remote_copy(
+            src_ref=grid_ref.at[pl.ds(0, PLANE), cols],
+            dst_ref=planes.at[away, :, cols],
+            send_sem=plane_send.at[half, step, away],
+            recv_sem=plane_recv.at[half, step, away],
+            device_id={"slab": slab_at(away)},
+            device_id_type=MESH,
+        )
+
+    def slot_copy(step):
+        return pltpu.make_async_remote_copy(
+            src_ref=slot_ref,
+            dst_ref=slots.at[step],
+            send_sem=slot_send.at[step],
+            recv_sem=slot_recv.at[step],
+            device_id={"grp": group_at(step)},
+            device_id_type=MESH,
+        )
+
+    def fwd_copy(half, step):
+        return pltpu.make_async_remote_copy(
+            src_ref=sent.at[half, step],
+            dst_ref=got.at[half, step],
+            send_sem=fwd_send.at[half, step],
+            recv_sem=fwd_recv.at[half, step],
+            device_id={"grp": group_at(step)},
+            device_id_type=MESH,
+        )
+
+    def back_copy(half, step):
+        return pltpu.make_async_remote_copy(
+            src_ref=back.at[half, step],
+            dst_ref=vals.at[half, step],
+            send_sem=back_send.at[half, step],
+            recv_sem=back_recv.at[half, step],
+            device_id={"grp": lax.rem(me + groups - step, groups)},
+            device_id_type=MESH,
+        )
+
+    def top_copy(half, step, away):
+        return pltpu.make_async_remote_copy(
+            src_ref=vals.at[half, step, pl.ds(0, PLANE), :],
+            dst_ref=tops.at[half, step, away],
+            send_sem=top_send.at[half, step, away],
+            recv_sem=top_recv.at[half, step, away],
+            device_id={"slab": slab_at(away)},
+            device_id_type=MESH,
+        )
+
+    for half in range(HALVES):
+        for step in order:
+            for away in range(1, slabs):
+                copy = plane_copy(half, step, away)
+                copy.start()
+                pending.append(copy)
+    for step in range(1, groups):
+        copy = slot_copy(step)
+        copy.start()
+        pending.append(copy)
+
+    fwd_weights = fwd_ref[...]
+    for half in range(HALVES):
+        for step in order:
+            for away in range(1, slabs):
+                plane_copy(half, step, away).wait_recv()
+            cols = columns(group_at(step), half)
+            edge = [planes[away, :, cols] for away in range(1, slabs)]
+            edge.append(jnp.zeros((PLANE, piece), jnp.float32))
+            scaled = mix(fwd_weights, grid_ref[:, cols], jnp.concatenate(edge, axis=0))
+            if step:
+                sent[half, step] = scaled
+                copy = fwd_copy(half, step)
+                copy.start()
+                pending.append(copy)
+            else:
+                got[half, step] = scaled
+
+    slot_ids = lax.broadcasted_iota(jnp.int32, (per_slab, rows), 0)
+    for step in [0] + order[:-1]:
+        if step:
+            slot_copy(step).wait_recv()
+            row_slots = slots[step, 0:1, :]
+        else:
+            row_slots = slot_ref[0:1, :]
+        hit = jnp.where(slot_ids == row_slots, 1.0, 0.0)
+        flat = hit.astype(jnp.bfloat16)
+        pick[step] = jnp.concatenate([flat, flat], axis=1)
+        turned = jnp.transpose(hit).astype(jnp.bfloat16)
+        place[step] = jnp.concatenate([turned, turned], axis=1)
+
+    for half in range(HALVES):
+        for count, step in enumerate([0] + order[:-1]):
+            if step:
+                fwd_copy(half, step).wait_recv()
+            high, low = split_pair(got[half, step])
+            term = jnp.dot(pick[step], jnp.concatenate([high, low], axis=0), preferred_element_type=jnp.float32)
+            table[...] = term if count == 0 else table[...] + term
+        high, low = split_pair(table[...])
+        spread[...] = jnp.concatenate([high, low], axis=0)
+        for step in order:
+            rebuilt = jnp.dot(place[step], spread[...], preferred_element_type=jnp.float32)
+            if step:
+                back[half, step] = rebuilt
+                copy = back_copy(half, step)
+                copy.start()
+                pending.append(copy)
+            else:
+                vals[half, step] = rebuilt
+
+    back_weights = back_ref[...]
+
+    def finish(half, step):
+        for away in range(1, slabs):
+            top_copy(half, step, away).wait_recv()
+        edge = [tops[half, step, away] for away in range(1, slabs)]
+        edge.append(jnp.zeros((PLANE, piece), jnp.float32))
+        out_ref[:, columns(group_at(step), half)] = mix(back_weights, vals[half, step], jnp.concatenate(edge, axis=0))
+
+    waiting = []
+    for half in range(HALVES):
+        for step in [0] + order[:-1]:
+            if step:
+                back_copy(half, step).wait_recv()
+            for away in range(1, slabs):
+                copy = top_copy(half, step, away)
+                copy.start()
+                pending.append(copy)
+            waiting.append((half, step))
+            if len(waiting) > 3:
+                finish(*waiting.pop(0))
+    for item in waiting:
+        finish(*item)
+    for copy in pending:
+        copy.wait_send()
+
+
+def fused_shards(grids, first_level, coeffs, slot_map):
+    grid_rows = grids[0]
+    level = first_level[0]
+    second = LEVEL_SUM - level
+    rows_dev, width = grid_rows.shape
+    slabs = lax.axis_size("slab")
+    groups = lax.axis_size("grp")
+    here = lax.axis_index("slab")
+    per_slab = 2 * ROWS // slabs
+    piece = width // (groups * HALVES)
+    span = rows_dev >> second
+    long = jnp.left_shift(1, level)
+    short = jnp.left_shift(1, second)
+    row_ids = jnp.arange(rows_dev, dtype=jnp.int32)
+    row_first = here * span + (row_ids >> second)
+    row_second = row_ids & short - 1
+    edge_ids = jnp.arange(slabs * PLANE, dtype=jnp.int32)
+    edge_away = edge_ids // PLANE + 1
+    edge_slab = (here + slabs - edge_away) % slabs
+    edge_first = edge_slab * span
+    edge_second = edge_ids % PLANE
+    edge_live = ((edge_away < slabs) & (edge_second < short)).astype(jnp.float32)
+
+    def weights(maker, factor):
+        body = maker(row_first[:, None], row_first[None, :], long) * maker(row_second[:, None], row_second[None, :], short)
+        edge = maker(row_first[:, None], edge_first[None, :], long) * maker(row_second[:, None], edge_second[None, :], short)
+        edge = edge * edge_live[None, :]
+        return (factor * jnp.concatenate([body, body, edge, edge], axis=1)).astype(jnp.bfloat16)
+
+    fwd_weights = weights(hier_weight, coeffs[0].astype(jnp.float32))
+    back_weights = weights(dehier_weight, 1.0)
+    slot_rows = jnp.broadcast_to(slot_map % per_slab, (PLANE, rows_dev))
+    f32, bf16 = jnp.float32, jnp.bfloat16
+    dma = pltpu.SemaphoreType.DMA
+    block = (HALVES, groups, rows_dev, piece)
+    in_vmem = pl.BlockSpec(memory_space=pltpu.VMEM)
+    result = pl.pallas_call(
+        functools.partial(kernel, groups, slabs, per_slab),
+        out_shape=jax.ShapeDtypeStruct((rows_dev, width), f32),
+        in_specs=[in_vmem] * 4,
+        out_specs=in_vmem,
+        scratch_shapes=[
+            pltpu.VMEM(block, f32),
+            pltpu.VMEM(block, f32),
+            pltpu.VMEM((per_slab, piece), f32),
+            pltpu.VMEM((2 * per_slab, piece), bf16),
+            pltpu.VMEM(block, f32),
+            pltpu.VMEM(block, f32),
+            pltpu.VMEM((slabs, PLANE, width), f32),
+            pltpu.VMEM((HALVES, groups, slabs, PLANE, piece), f32),
+            pltpu.VMEM((groups, PLANE, rows_dev), jnp.int32),
+            pltpu.VMEM((groups, per_slab, 2 * rows_dev), bf16),
+            pltpu.VMEM((groups, rows_dev, 2 * per_slab), bf16),
+            dma((HALVES, groups, slabs)),
+            dma((HALVES, groups, slabs)),
+            dma((groups,)),
+            dma((groups,)),
+            dma((HALVES, groups)),
+            dma((HALVES, groups)),
+            dma((HALVES, groups)),
+            dma((HALVES, groups)),
+            dma((HALVES, groups, slabs)),
+            dma((HALVES, groups, slabs)),
+        ],
+        compiler_params=pltpu.CompilerParams(collective_id=0, has_side_effects=True, vmem_limit_bytes=40 << 20),
+    )(grid_rows, slot_rows, fwd_weights, back_weights)
+    return result[None]
+
+
 def solution(mesh):
     in_specs = (P("grp", "slab", None), P("grp"), P("grp"), P("grp", "slab"))
     out_specs = P("grp", "slab", None)
-    return jax.shard_map(shards, mesh=mesh, in_specs=in_specs, out_specs=out_specs, check_vma=False)
+
+    def whole(grids, first_level, coeffs, slot_map):
+        groups, rows, width = grids.shape
+        few = mesh.shape["grp"] == groups and groups * rows <= 4 * 2 * ROWS
+        even = width % (groups * HALVES * LANES) == 0 and rows // mesh.shape["slab"] == LANES
+        body = fused_shards if few and even else shards
+        step = jax.shard_map(body, mesh=mesh, in_specs=in_specs, out_specs=out_specs, check_vma=False)
+        return step(grids, first_level, coeffs, slot_map)
+
+    return whole

time: 231 us -> 114 us (0.49)
  waiting for transfers between devices: 156 us -> 0 us
  Pallas kernels: 0 us -> 108 us
  matrix products: 35.2 us -> 0 us
  blocking collectives: 16 us -> 0 us
  between operations: 15 us -> 1.41 us
  local copies, waits for them, and re-layouts: 6.43 us -> 2.91 us
    psum x1 -> x0, waiting for transfers between devices: 156 us -> none  [shards(): total = lax.psum(term, 'grp')]
    pallas_call x0 -> x1, Pallas kernels: none -> 108 us  [fused_shards(): pl.pallas_call(functools.partial(kernel, groups, slabs, per_slab), out_sh...]
    dot_general x15 -> x0, matrix products: 35.2 us -> none  [the longest x8 20.9 us: exact_dot(): jnp.dot(left, right, precision=lax.Precision.HIGHEST, preferred_element_t...]
    all_gather x2 -> x0, blocking collectives: 16 us -> none  [the longest x1 8.82 us: shards(): planes = lax.all_gather(plane[None], 'slab', axis=0, tiled=True)]
    mul x2 -> x0, local copies, waits for them, and re-layouts: 3.38 us -> none  [the longest x1 2.44 us: shards(): jnp.kron(square_table(hier_weight, P3), square_table(hier_weight, P4))]
  transfers between devices with their start and end apart: 1 -> 0, of which waited for: 1 -> 0; matrix products, arithmetic and copies ran while one was open for 1% -> 0% of each run, Pallas kernels for 0% -> 0%
where the time goes in v1:
time: 114 us
  Pallas kernels  108 us (95%)
  local copies, waits for them, and re-layouts  2.91 us (3%)
  other arithmetic  1.59 us (1%)
  between operations  1.41 us (1%)
    pallas_call x1, Pallas kernels, fused_shards(): pl.pallas_call(functools.partial(kernel, groups, slabs, per_slab), out_sh...  108 us
    unnamed x3, local copies, waits for them, and re-layouts  2.91 us

profile of v1, /device:TPU:0, one launch (start us, length us, event | category | flops | bytes accessed | tf_op | source)
XLA Modules:
  0.0 114.0 jit_solution(10640065066854703188)
XLA Ops:
  1.3 0.1 and_select_fusion.3
  1.5 0.7 fusion.31
  2.2 0.1 maximum_convert_fusion.1
  2.4 0.2 fusion.24
  2.6 0.2 fusion.25
  2.8 0.1 fusion.fwd_ref
  2.9 0.1 pad_maximum_fusion.back_ref
  3.0 0.0 copy-start
  3.0 1.6 %copy-done = f32[1,128,4096]{2,1,0:T(8,128)S(1)} copy-done((f32[1,128,4096]{2,1,0:T(8,128)S(1)}, f32[1,128,4096]{2,1,0:T(8,128)}, u32[]{:S(2)}) %copy-start) | copy-done | bytes 2097176
  4.6 108.1 %shard_map.46 = f32[128,4096]{1,0:T(8,128)S(1)} custom-call(f32[128,4096]{1,0:T(8,128)S(1)} %bitcast.8, s32[8,128]{1,0:T(8,128)S(1)} %broadcast_in_dim.65.slot_ref, bf16[128,320]{1,0:T(8,128)(2,1)S(1)} %fusion.fwd_ref, bf16[128,320]{1,0:T(8,128)(2,1)S(1)} %pad_maximum_fusion.back_ref), custom_call_target="tpu_custom_call" | custom-call | tf_op jit(solution)/shard_map/pallas_call | solution.py:343
  112.6 1.3 %copy.16 = f32[1,128,4096]{2,1,0:T(8,128)} copy(f32[1,128,4096]{2,1,0:T(8,128)S(1)} %bitcast.7) | data formatting | bytes 4194304
  (9 shorter events, 0.1 us)
Async XLA Ops:
  3.0 1.6 %copy-start = (f32[1,128,4096]{2,1,0:T(8,128)S(1)}, f32[1,128,4096]{2,1,0:T(8,128)}, u32[]{:S(2)}) copy-start(f32[1,128,4096]{2,1,0:T(8,128)} %param.4) | copy-start | bytes 6291460

commit v2 on v0

--- a/solution.py
+++ b/solution.py
@@ -1,6 +1,10 @@
+import functools
+
 import jax
 import jax.numpy as jnp
 from jax import lax
+from jax.experimental import pallas as pl
+from jax.experimental.pallas import tpu as pltpu
 from jax.sharding import PartitionSpec as P
 
 P2 = 16
@@ -9,6 +13,7 @@
 LEVEL_SUM = 9
 PLANE = 8
 ROWS = 512
+MESH = pl.DeviceIdType.MESH
 
 
 def hier_weight(target, source, period):
@@ -115,7 +120,317 @@
     return nodal[None]
 
 
+PAIR = 2
+LANES = 128
+PACK = 4
+LAG = 2
+HOP = 2
+
+
+def split_pair(values):
+    high = values.astype(jnp.bfloat16)
+    low = (values - high.astype(jnp.float32)).astype(jnp.bfloat16)
+    return high, low
+
+
+def mix(weights, body, edge):
+    body_high, body_low = split_pair(body)
+    edge_high, edge_low = split_pair(edge)
+    stacked = jnp.concatenate([body_high, body_low, edge_high, edge_low], axis=0)
+    return jnp.dot(weights, stacked, preferred_element_type=jnp.float32)
+
+
+def kernel(groups, slabs, per_slab, grid_ref, slot_ref, fwd_ref, back_ref, out_ref,
+           mine, sent, got, own, pre, suf, pre_out, suf_out, back, vals, planes, tops, slots, pick, place,
+           plane_send, plane_recv, slot_sems, y_send, y_recv, pre_send, pre_recv, suf_send, suf_recv,
+           back_send, back_recv, top_send, top_recv):
+    me = lax.axis_index("grp")
+    here = lax.axis_index("slab")
+    rows, width = grid_ref.shape
+    chunks = own.shape[0]
+    piece = own.shape[2]
+    side = lax.rem(me, PAIR)
+    line = me // PAIR
+    length = groups // PAIR
+    partner = me + 1 - 2 * side
+    right = lax.rem(me + PAIR, groups)
+    left = lax.rem(me + groups - PAIR, groups)
+    half = width // PAIR
+
+    def slab_at(step):
+        return lax.rem(here + step, slabs)
+
+    def columns(other, chunk):
+        base = (side if other == 0 else 1 - side) * half
+        return pl.ds(pl.multiple_of(base + chunk * piece, piece), piece)
+
+    def remote(src, dst, send, recv, axis, target):
+        return pltpu.make_async_remote_copy(
+            src_ref=src, dst_ref=dst, send_sem=send, recv_sem=recv,
+            device_id={axis: target}, device_id_type=MESH,
+        )
+
+    barrier = pltpu.get_barrier_semaphore()
+    for target in (partner, left, right):
+        pl.semaphore_signal(barrier, inc=1, device_id={"grp": target}, device_id_type=MESH)
+    for step in range(1, slabs):
+        pl.semaphore_signal(barrier, inc=1, device_id={"slab": slab_at(step)}, device_id_type=MESH)
+    pl.semaphore_wait(barrier, slabs + 2)
+
+    packs = chunks // PACK
+
+    def plane_copy(other, pack, away):
+        base = (side if other == 0 else 1 - side) * half
+        cols = pl.ds(pl.multiple_of(base + pack * PACK * piece, piece), PACK * piece)
+        return remote(grid_ref.at[pl.ds(0, PLANE), cols], planes.at[away, :, cols],
+                      plane_send.at[other, pack, away], plane_recv.at[other, pack, away], "slab", slab_at(away))
+
+    def y_copy(c):
+        return remote(sent.at[c], got.at[c], y_send.at[c], y_recv.at[c], "grp", partner)
+
+    def pre_copy(c):
+        return remote(pre_out.at[c], pre.at[c], pre_send.at[c], pre_recv.at[c], "grp", right)
+
+    def suf_copy(c):
+        return remote(suf_out.at[c], suf.at[c], suf_send.at[c], suf_recv.at[c], "grp", left)
+
+    def back_copy(c):
+        return remote(back.at[c], vals.at[1, c], back_send.at[c], back_recv.at[c], "grp", partner)
+
+    def top_copy(other, c, away):
+        return remote(vals.at[other, c, pl.ds(0, PLANE), :], tops.at[other, c, away],
+                      top_send.at[other, c, away], top_recv.at[other, c, away], "slab", slab_at(away))
+
+    slot_copy = remote(slot_ref, slots, slot_sems.at[0], slot_sems.at[1], "grp", partner)
+
+    for pack in range(packs):
+        for other in (1, 0):
+            for away in range(1, slabs):
+                plane_copy(other, pack, away).start()
+        if pack == 0:
+            slot_copy.start()
+
+    @pl.when(line == 0)
+    def _():
+        pre[...] = jnp.zeros_like(pre)
+
+    @pl.when(line == length - 1)
+    def _():
+        suf[...] = jnp.zeros_like(suf)
+
+    slot_ids = lax.broadcasted_iota(jnp.int32, (per_slab, rows), 0)
+
+    def fill(index, row_slots):
+        hit = jnp.where(slot_ids == row_slots, 1.0, 0.0)
+        flat = hit.astype(jnp.bfloat16)
+        pick[index] = jnp.concatenate([flat, flat], axis=1)
+        turned = jnp.transpose(hit).astype(jnp.bfloat16)
+        place[index] = jnp.concatenate([turned, turned], axis=1)
+
+    fill(0, slot_ref[0:1, :])
+
+    def scaled(other, c):
+        cols = columns(other, c)
+        edge = [planes[away, :, cols] for away in range(1, slabs)]
+        edge.append(jnp.zeros((PLANE, piece), jnp.float32))
+        return mix(fwd_ref[...], grid_ref[:, cols], jnp.concatenate(edge, axis=0))
+
+    def at(c, body):
+        pl.when((c >= 0) & (c < chunks))(lambda: body(c))
+
+    def start(c):
+        @pl.when(lax.rem(c, PACK) == 0)
+        def _():
+            for other in (1, 0):
+                for away in range(1, slabs):
+                    plane_copy(other, c // PACK, away).wait_recv()
+
+        sent[c] = scaled(1, c)
+        y_copy(c).start()
+        mine[c] = scaled(0, c)
+
+    def merge(c):
+        high, low = split_pair(mine[c])
+        first = jnp.dot(pick[0], jnp.concatenate([high, low], axis=0), preferred_element_type=jnp.float32)
+        y_copy(c).wait_recv()
+        high, low = split_pair(got[c])
+        own[c] = first + jnp.dot(pick[1], jnp.concatenate([high, low], axis=0), preferred_element_type=jnp.float32)
+
+    def from_left(c):
+        @pl.when(line > 0)
+        def _():
+            pre_copy(c).wait_recv()
+
+        @pl.when(line < length - 1)
+        def _():
+            pre_out[c] = pre[c] + own[c]
+            pre_copy(c).start()
+
+    def from_right(c):
+        @pl.when(line < length - 1)
+        def _():
+            suf_copy(c).wait_recv()
+
+        @pl.when(line > 0)
+        def _():
+            suf_out[c] = suf[c] + own[c]
+            suf_copy(c).start()
+
+    def rebuild(c):
+        high, low = split_pair(pre[c] + own[c] + suf[c])
+        both = jnp.concatenate([high, low], axis=0)
+        back[c] = jnp.dot(place[1], both, preferred_element_type=jnp.float32)
+        back_copy(c).start()
+        vals[0, c] = jnp.dot(place[0], both, preferred_element_type=jnp.float32)
+
+    def share(c):
+        for away in range(1, slabs):
+            top_copy(0, c, away).start()
+        back_copy(c).wait_recv()
+        for away in range(1, slabs):
+            top_copy(1, c, away).start()
+
+    def finish(c):
+        for other in range(2):
+            for away in range(1, slabs):
+                top_copy(other, c, away).wait_recv()
+            edge = [tops[other, c, away] for away in range(1, slabs)]
+            edge.append(jnp.zeros((PLANE, piece), jnp.float32))
+            out_ref[:, columns(other, c)] = mix(back_ref[...], vals[other, c], jnp.concatenate(edge, axis=0))
+
+    def round_of(t, carry):
+        at(t, start)
+
+        @pl.when(t == 0)
+        def _():
+            slot_copy.wait_recv()
+            fill(1, slots[0:1, :])
+
+        ready = t - LAG
+        at(ready, merge)
+        at(ready - HOP * line, from_left)
+        at(ready - HOP * (length - 1 - line), from_right)
+        done = ready - HOP * jnp.maximum(line, length - 1 - line)
+        at(done, rebuild)
+        at(done - LAG, share)
+        at(done - LAG - 1, finish)
+        return carry
+
+    lax.fori_loop(0, chunks + 2 * LAG + 1 + HOP * (length - 1), round_of, 0)
+
+    def drain(c, carry):
+        y_copy(c).wait_send()
+        back_copy(c).wait_send()
+
+        @pl.when(line < length - 1)
+        def _():
+            pre_copy(c).wait_send()
+
+        @pl.when(line > 0)
+        def _():
+            suf_copy(c).wait_send()
+
+        for other in range(2):
+            for away in range(1, slabs):
+                top_copy(other, c, away).wait_send()
+        return carry
+
+    lax.fori_loop(0, chunks, drain, 0)
+    for pack in range(packs):
+        for other in range(2):
+            for away in range(1, slabs):
+                plane_copy(other, pack, away).wait_send()
+    slot_copy.wait_send()
+
+
+def fused_shards(grids, first_level, coeffs, slot_map):
+    grid_rows = grids[0]
+    level = first_level[0]
+    second = LEVEL_SUM - level
+    rows_dev, width = grid_rows.shape
+    slabs = lax.axis_size("slab")
+    groups = lax.axis_size("grp")
+    here = lax.axis_index("slab")
+    per_slab = 2 * ROWS // slabs
+    piece = LANES
+    chunks = width // (PAIR * piece)
+    span = rows_dev >> second
+    long = jnp.left_shift(1, level)
+    short = jnp.left_shift(1, second)
+    row_ids = jnp.arange(rows_dev, dtype=jnp.int32)
+    row_first = here * span + (row_ids >> second)
+    row_second = row_ids & short - 1
+    edge_ids = jnp.arange(slabs * PLANE, dtype=jnp.int32)
+    edge_away = edge_ids // PLANE + 1
+    edge_slab = (here + slabs - edge_away) % slabs
+    edge_first = edge_slab * span
+    edge_second = edge_ids % PLANE
+    edge_live = ((edge_away < slabs) & (edge_second < short)).astype(jnp.float32)
+
+    def weights(maker, factor):
+        body = maker(row_first[:, None], row_first[None, :], long) * maker(row_second[:, None], row_second[None, :], short)
+        edge = maker(row_first[:, None], edge_first[None, :], long) * maker(row_second[:, None], edge_second[None, :], short)
+        edge = edge * edge_live[None, :]
+        return (factor * jnp.concatenate([body, body, edge, edge], axis=1)).astype(jnp.bfloat16)
+
+    fwd_weights = weights(hier_weight, coeffs[0].astype(jnp.float32))
+    back_weights = weights(dehier_weight, 1.0)
+    slot_rows = jnp.broadcast_to(slot_map % per_slab, (PLANE, rows_dev))
+    f32, bf16 = jnp.float32, jnp.bfloat16
+    dma = pltpu.SemaphoreType.DMA
+    short_block = (chunks, rows_dev, piece)
+    tall_block = (chunks, per_slab, piece)
+    in_vmem = pl.BlockSpec(memory_space=pltpu.VMEM)
+    result = pl.pallas_call(
+        functools.partial(kernel, groups, slabs, per_slab),
+        out_shape=jax.ShapeDtypeStruct((rows_dev, width), f32),
+        in_specs=[in_vmem] * 4,
+        out_specs=in_vmem,
+        scratch_shapes=[
+            pltpu.VMEM(short_block, f32),
+            pltpu.VMEM(short_block, f32),
+            pltpu.VMEM(short_block, f32),
+            pltpu.VMEM(tall_block, f32),
+            pltpu.VMEM(tall_block, f32),
+            pltpu.VMEM(tall_block, f32),
+            pltpu.VMEM(tall_block, f32),
+            pltpu.VMEM(tall_block, f32),
+            pltpu.VMEM(short_block, f32),
+            pltpu.VMEM((2,) + short_block, f32),
+            pltpu.VMEM((slabs, PLANE, width), f32),
+            pltpu.VMEM((2, chunks, slabs, PLANE, piece), f32),
+            pltpu.VMEM((PLANE, rows_dev), jnp.int32),
+            pltpu.VMEM((2, per_slab, 2 * rows_dev), bf16),
+            pltpu.VMEM((2, rows_dev, 2 * per_slab), bf16),
+            dma((2, chunks // PACK, slabs)),
+            dma((2, chunks // PACK, slabs)),
+            dma((2,)),
+            dma((chunks,)),
+            dma((chunks,)),
+            dma((chunks,)),
+            dma((chunks,)),
+            dma((chunks,)),
+            dma((chunks,)),
+            dma((chunks,)),
+            dma((chunks,)),
+            dma((2, chunks, slabs)),
+            dma((2, chunks, slabs)),
+        ],
+        compiler_params=pltpu.CompilerParams(collective_id=0, has_side_effects=True, vmem_limit_bytes=40 << 20),
+    )(grid_rows, slot_rows, fwd_weights, back_weights)
+    return result[None]
+
+
 def solution(mesh):
     in_specs = (P("grp", "slab", None), P("grp"), P("grp"), P("grp", "slab"))
     out_specs = P("grp", "slab", None)
-    return jax.shard_map(shards, mesh=mesh, in_specs=in_specs, out_specs=out_specs, check_vma=False)
+
+    def whole(grids, first_level, coeffs, slot_map):
+        groups, rows, width = grids.shape
+        few = mesh.shape["grp"] == groups and groups * rows <= 4 * 2 * ROWS
+        even = groups % PAIR == 0 and groups > PAIR and width % (PAIR * PACK * LANES) == 0 and rows // mesh.shape["slab"] == LANES
+        body = fused_shards if few and even else shards
+        step = jax.shard_map(body, mesh=mesh, in_specs=in_specs, out_specs=out_specs, check_vma=False)
+        return step(grids, first_level, coeffs, slot_map)
+
+    return whole

time: 231 us -> 87.9 us (0.38)
  waiting for transfers between devices: 156 us -> 0 us
  Pallas kernels: 0 us -> 81.8 us
  matrix products: 35.2 us -> 0 us
  blocking collectives: 16 us -> 0 us
  between operations: 15 us -> 1.41 us
  local copies, waits for them, and re-layouts: 6.43 us -> 2.91 us
    psum x1 -> x0, waiting for transfers between devices: 156 us -> none  [shards(): total = lax.psum(term, 'grp')]
    pallas_call x0 -> x1, Pallas kernels: none -> 81.8 us  [fused_shards(): pl.pallas_call(functools.partial(kernel, groups, slabs, per_slab), out_sh...]
    dot_general x15 -> x0, matrix products: 35.2 us -> none  [the longest x8 20.9 us: exact_dot(): jnp.dot(left, right, precision=lax.Precision.HIGHEST, preferred_element_t...]
    all_gather x2 -> x0, blocking collectives: 16 us -> none  [the longest x1 8.82 us: shards(): planes = lax.all_gather(plane[None], 'slab', axis=0, tiled=True)]
    mul x2 -> x0, local copies, waits for them, and re-layouts: 3.38 us -> none  [the longest x1 2.44 us: shards(): jnp.kron(square_table(hier_weight, P3), square_table(hier_weight, P4))]
  transfers between devices with their start and end apart: 1 -> 0, of which waited for: 1 -> 0; matrix products, arithmetic and copies ran while one was open for 1% -> 0% of each run, Pallas kernels for 0% -> 0%
where the time goes in v2:
time: 87.9 us; the launch traced here: 87.7 us
  Pallas kernels  81.8 us (93%)
  local copies, waits for them, and re-layouts  2.91 us (3%)
  other arithmetic  1.59 us (2%)
  between operations  1.41 us (2%)
    pallas_call x1, Pallas kernels, fused_shards(): pl.pallas_call(functools.partial(kernel, groups, slabs, per_slab), out_sh...  81.8 us
    unnamed x3, local copies, waits for them, and re-layouts  2.91 us

profile of v2, /device:TPU:0, one launch (start us, length us, event | category | flops | bytes accessed | tf_op | source)
XLA Modules:
  0.0 87.7 jit_solution(14148912469059811366)
XLA Ops:
  1.3 0.1 and_select_fusion.3
  1.5 0.7 fusion.31
  2.2 0.1 maximum_convert_fusion.1
  2.4 0.2 fusion.24
  2.6 0.2 fusion.25
  2.8 0.1 fusion.fwd_ref
  2.9 0.1 pad_maximum_fusion.back_ref
  3.0 0.0 copy-start
  3.0 1.6 %copy-done = f32[1,128,4096]{2,1,0:T(8,128)S(1)} copy-done((f32[1,128,4096]{2,1,0:T(8,128)S(1)}, f32[1,128,4096]{2,1,0:T(8,128)}, u32[]{:S(2)}) %copy-start) | copy-done | bytes 2097176
  4.6 81.8 %shard_map.46 = f32[128,4096]{1,0:T(8,128)S(1)} custom-call(f32[128,4096]{1,0:T(8,128)S(1)} %bitcast.8, s32[8,128]{1,0:T(8,128)S(1)} %broadcast_in_dim.65.slot_ref, bf16[128,320]{1,0:T(8,128)(2,1)S(1)} %fusion.fwd_ref, bf16[128,320]{1,0:T(8,128)(2,1)S(1)} %pad_maximum_fusion.back_ref), custom_call_target="tpu_custom_call" | custom-call | tf_op jit(solution)/shard_map/pallas_call | solution.py:384
  86.4 1.3 %copy.16 = f32[1,128,4096]{2,1,0:T(8,128)} copy(f32[1,128,4096]{2,1,0:T(8,128)S(1)} %bitcast.7) | data formatting | bytes 4194304
  (9 shorter events, 0.1 us)
Async XLA Ops:
  3.0 1.6 %copy-start = (f32[1,128,4096]{2,1,0:T(8,128)S(1)}, f32[1,128,4096]{2,1,0:T(8,128)}, u32[]{:S(2)}) copy-start(f32[1,128,4096]{2,1,0:T(8,128)} %param.4) | copy-start | bytes 6291460

commit v3 on v2

--- a/solution.py
+++ b/solution.py
@@ -125,6 +125,7 @@
 PACK = 4
 LAG = 2
 HOP = 2
+PARTS = 2
 
 
 def split_pair(values):
@@ -188,11 +189,16 @@
     def y_copy(c):
         return remote(sent.at[c], got.at[c], y_send.at[c], y_recv.at[c], "grp", partner)
 
-    def pre_copy(c):
-        return remote(pre_out.at[c], pre.at[c], pre_send.at[c], pre_recv.at[c], "grp", right)
-
-    def suf_copy(c):
-        return remote(suf_out.at[c], suf.at[c], suf_send.at[c], suf_recv.at[c], "grp", left)
+    def share_of(part):
+        return pl.ds(part * (per_slab // PARTS), per_slab // PARTS)
+
+    def pre_copy(c, part):
+        return remote(pre_out.at[c, share_of(part)], pre.at[c, share_of(part)],
+                      pre_send.at[c, part], pre_recv.at[c, part], "grp", right)
+
+    def suf_copy(c, part):
+        return remote(suf_out.at[c, share_of(part)], suf.at[c, share_of(part)],
+                      suf_send.at[c, part], suf_recv.at[c, part], "grp", left)
 
     def back_copy(c):
         return remote(back.at[c], vals.at[1, c], back_send.at[c], back_recv.at[c], "grp", partner)
@@ -223,17 +229,15 @@
     def fill(index, row_slots):
         hit = jnp.where(slot_ids == row_slots, 1.0, 0.0)
         flat = hit.astype(jnp.bfloat16)
-        pick[index] = jnp.concatenate([flat, flat], axis=1)
+        for copy in range(2):
+            pick[:, pl.ds((2 * copy + index) * rows, rows)] = flat
         turned = jnp.transpose(hit).astype(jnp.bfloat16)
-        place[index] = jnp.concatenate([turned, turned], axis=1)
+        place[pl.ds(index * rows, rows), :] = jnp.concatenate([turned, turned], axis=1)
 
     fill(0, slot_ref[0:1, :])
 
-    def scaled(other, c):
-        cols = columns(other, c)
-        edge = [planes[away, :, cols] for away in range(1, slabs)]
-        edge.append(jnp.zeros((PLANE, piece), jnp.float32))
-        return mix(fwd_ref[...], grid_ref[:, cols], jnp.concatenate(edge, axis=0))
+    def edges(parts):
+        return jnp.concatenate(parts + [jnp.zeros((PLANE, piece), jnp.float32)], axis=0)
 
     def at(c, body):
         pl.when((c >= 0) & (c < chunks))(lambda: body(c))
@@ -245,43 +249,48 @@
                 for away in range(1, slabs):
                     plane_copy(other, c // PACK, away).wait_recv()
 
-        sent[c] = scaled(1, c)
+        both = [columns(1, c), columns(0, c)]
+        body = jnp.concatenate([grid_ref[:, cols] for cols in both], axis=1)
+        edge = [edges([planes[away, :, cols] for away in range(1, slabs)]) for cols in both]
+        scaled = mix(fwd_ref[...], body, jnp.concatenate(edge, axis=1))
+        sent[c] = scaled[:, :piece]
         y_copy(c).start()
-        mine[c] = scaled(0, c)
+        mine[c] = scaled[:, piece:]
 
     def merge(c):
-        high, low = split_pair(mine[c])
-        first = jnp.dot(pick[0], jnp.concatenate([high, low], axis=0), preferred_element_type=jnp.float32)
         y_copy(c).wait_recv()
-        high, low = split_pair(got[c])
-        own[c] = first + jnp.dot(pick[1], jnp.concatenate([high, low], axis=0), preferred_element_type=jnp.float32)
+        high, low = split_pair(jnp.concatenate([mine[c], got[c]], axis=0))
+        own[c] = jnp.dot(pick[...], jnp.concatenate([high, low], axis=0), preferred_element_type=jnp.float32)
 
     def from_left(c):
-        @pl.when(line > 0)
-        def _():
-            pre_copy(c).wait_recv()
-
-        @pl.when(line < length - 1)
-        def _():
-            pre_out[c] = pre[c] + own[c]
-            pre_copy(c).start()
+        for part in range(PARTS):
+            @pl.when(line > 0)
+            def _():
+                pre_copy(c, part).wait_recv()
+
+            @pl.when(line < length - 1)
+            def _():
+                pre_out[c, share_of(part)] = pre[c, share_of(part)] + own[c, share_of(part)]
+                pre_copy(c, part).start()
 
     def from_right(c):
-        @pl.when(line < length - 1)
-        def _():
-            suf_copy(c).wait_recv()
-
-        @pl.when(line > 0)
-        def _():
-            suf_out[c] = suf[c] + own[c]
-            suf_copy(c).start()
+        for part in range(PARTS):
+            @pl.when(line < length - 1)
+            def _():
+                suf_copy(c, part).wait_recv()
+
+            @pl.when(line > 0)
+            def _():
+                suf_out[c, share_of(part)] = suf[c, share_of(part)] + own[c, share_of(part)]
+                suf_copy(c, part).start()
 
     def rebuild(c):
         high, low = split_pair(pre[c] + own[c] + suf[c])
         both = jnp.concatenate([high, low], axis=0)
-        back[c] = jnp.dot(place[1], both, preferred_element_type=jnp.float32)
+        placed = jnp.dot(place[...], both, preferred_element_type=jnp.float32)
+        back[c] = placed[rows:]
         back_copy(c).start()
-        vals[0, c] = jnp.dot(place[0], both, preferred_element_type=jnp.float32)
+        vals[0, c] = placed[:rows]
 
     def share(c):
         for away in range(1, slabs):
@@ -291,12 +300,15 @@
             top_copy(1, c, away).start()
 
     def finish(c):
+        edge = []
         for other in range(2):
             for away in range(1, slabs):
                 top_copy(other, c, away).wait_recv()
-            edge = [tops[other, c, away] for away in range(1, slabs)]
-            edge.append(jnp.zeros((PLANE, piece), jnp.float32))
-            out_ref[:, columns(other, c)] = mix(back_ref[...], vals[other, c], jnp.concatenate(edge, axis=0))
+            edge.append(edges([tops[other, c, away] for away in range(1, slabs)]))
+        body = jnp.concatenate([vals[0, c], vals[1, c]], axis=1)
+        nodal = mix(back_ref[...], body, jnp.concatenate(edge, axis=1))
+        out_ref[:, columns(0, c)] = nodal[:, :piece]
+        out_ref[:, columns(1, c)] = nodal[:, piece:]
 
     def round_of(t, carry):
         at(t, start)
@@ -324,11 +336,13 @@
 
         @pl.when(line < length - 1)
         def _():
-            pre_copy(c).wait_send()
+            for part in range(PARTS):
+                pre_copy(c, part).wait_send()
 
         @pl.when(line > 0)
         def _():
-            suf_copy(c).wait_send()
+            for part in range(PARTS):
+                suf_copy(c, part).wait_send()
 
         for other in range(2):
             for away in range(1, slabs):
@@ -400,17 +414,17 @@
             pltpu.VMEM((slabs, PLANE, width), f32),
             pltpu.VMEM((2, chunks, slabs, PLANE, piece), f32),
             pltpu.VMEM((PLANE, rows_dev), jnp.int32),
-            pltpu.VMEM((2, per_slab, 2 * rows_dev), bf16),
-            pltpu.VMEM((2, rows_dev, 2 * per_slab), bf16),
+            pltpu.VMEM((per_slab, 4 * rows_dev), bf16),
+            pltpu.VMEM((2 * rows_dev, 2 * per_slab), bf16),
             dma((2, chunks // PACK, slabs)),
             dma((2, chunks // PACK, slabs)),
             dma((2,)),
             dma((chunks,)),
             dma((chunks,)),
-            dma((chunks,)),
-            dma((chunks,)),
-            dma((chunks,)),
-            dma((chunks,)),
+            dma((chunks, PARTS)),
+            dma((chunks, PARTS)),
+            dma((chunks, PARTS)),
+            dma((chunks, PARTS)),
             dma((chunks,)),
             dma((chunks,)),
             dma((2, chunks, slabs)),

time: 87.9 us -> 88.2 us (level)
  no operation moved by 1% of the time
where the time goes in v3:
time: 88.2 us; the launch traced here: 88 us
  Pallas kernels  82.1 us (93%)
  local copies, waits for them, and re-layouts  2.91 us (3%)
  other arithmetic  1.59 us (2%)
  between operations  1.41 us (2%)
    pallas_call x1, Pallas kernels, fused_shards(): pl.pallas_call(functools.partial(kernel, groups, slabs, per_slab), out_sh...  82.1 us
    unnamed x3, local copies, waits for them, and re-layouts  2.91 us

profile of v3, /device:TPU:0, one launch (start us, length us, event | category | flops | bytes accessed | tf_op | source)
XLA Modules:
  0.0 88.0 jit_solution(9954149928562504120)
XLA Ops:
  1.3 0.1 and_select_fusion.3
  1.5 0.7 fusion.31
  2.2 0.1 maximum_convert_fusion.1
  2.4 0.2 fusion.24
  2.6 0.2 fusion.25
  2.8 0.1 fusion.fwd_ref
  2.9 0.1 pad_maximum_fusion.back_ref
  3.0 0.0 copy-start
  3.0 1.6 %copy-done = f32[1,128,4096]{2,1,0:T(8,128)S(1)} copy-done((f32[1,128,4096]{2,1,0:T(8,128)S(1)}, f32[1,128,4096]{2,1,0:T(8,128)}, u32[]{:S(2)}) %copy-start) | copy-done | bytes 2097176
  4.6 82.1 %shard_map.46 = f32[128,4096]{1,0:T(8,128)S(1)} custom-call(f32[128,4096]{1,0:T(8,128)S(1)} %bitcast.8, s32[8,128]{1,0:T(8,128)S(1)} %broadcast_in_dim.65.slot_ref, bf16[128,320]{1,0:T(8,128)(2,1)S(1)} %fusion.fwd_ref, bf16[128,320]{1,0:T(8,128)(2,1)S(1)} %pad_maximum_fusion.back_ref), custom_call_target="tpu_custom_call" | custom-call | tf_op jit(solution)/shard_map/pallas_call | solution.py:398
  86.7 1.3 %copy.16 = f32[1,128,4096]{2,1,0:T(8,128)} copy(f32[1,128,4096]{2,1,0:T(8,128)S(1)} %bitcast.7) | data formatting | bytes 4194304
  (9 shorter events, 0.1 us)
Async XLA Ops:
  3.0 1.6 %copy-start = (f32[1,128,4096]{2,1,0:T(8,128)S(1)}, f32[1,128,4096]{2,1,0:T(8,128)}, u32[]{:S(2)}) copy-start(f32[1,128,4096]{2,1,0:T(8,128)} %param.4) | copy-start | bytes 6291460
